TPU v7x, 128 devices: a whole 4x4x4 slice. The times are simulated.
128 devices in a mesh: dp: 16 (over y, x), row: 2 (over core), col: 4 (over z).
Axes of the slice: x: 4, y: 4, z: 4, core: 2. Of those that a mesh axis runs over, the one named last changes fastest.
Arguments:
- tokens: bfloat16 [15360, 4096], P(('dp', 'col'), 'row'), may hold values from -6 to 6
- hidden_cot: bfloat16 [15360, 14336], P(('dp', 'row'), 'col'), may hold values from -0.048339844 to 0.048339844
- gate_pre: bfloat16 [15360, 14336], P(('dp', 'row'), 'col'), may hold values from -10 to 10
- up_pre: bfloat16 [15360, 14336], P(('dp', 'row'), 'col'), may hold values from -6 to 6
Outputs:
- grad_gate: bfloat16 [2, 2048, 14336], P('row', 'dp', 'col')
All inputs are finite; a program needn't handle non-finite values.
Results may differ from a plain program's by a relative error of at most 0.014.
Values may be sent and summed in bfloat16 or wider, within the bound.
A program may use at most 128 MiB of HBM per device.

v0:
```python
import jax
import jax.numpy as jnp
from jax import lax
from jax.sharding import PartitionSpec as P


def copy_for_each(x, axis):
    copies = jnp.broadcast_to(x, (lax.axis_size(axis), *x.shape))
    return lax.all_to_all(copies, axis, split_axis=0, concat_axis=0, tiled=True)


def in_order(tiles, dim):
    lengths = list(tiles.shape[1:])
    lengths[dim] *= tiles.shape[0]
    return jnp.moveaxis(tiles, 0, dim).reshape(lengths)


def gather_directly(x, axis, dim):
    tiles = copy_for_each(x, axis)
    return in_order(tiles, dim)


def contract_rows(left, right):
    return lax.dot_general(
        left, right, (((0,), (0,)), ((), ())), preferred_element_type=jnp.float32
    )


def on_device(tokens, hidden_cot, gate_pre, up_pre):
    tok_full = lax.all_gather(tokens, "col", axis=0, tiled=True)
    gate_val = gate_pre.astype(jnp.float32)
    up_val = up_pre.astype(jnp.float32)
    cot_val = hidden_cot.astype(jnp.float32)
    sigma = jax.nn.sigmoid(gate_val)
    gate_grad = (cot_val * up_val * sigma * (1.0 + gate_val * (1.0 - sigma))).astype(jnp.bfloat16)
    group_part = contract_rows(tok_full, gather_directly(gate_grad, "row", 0))
    summed = lax.psum_scatter(
        group_part.astype(jnp.bfloat16), "dp", scatter_dimension=0, tiled=True
    )
    return summed.reshape(1, summed.shape[0], summed.shape[1])


def solution(mesh):
    in_specs = (
        P(("dp", "col"), "row"),
        P(("dp", "row"), "col"),
        P(("dp", "row"), "col"),
        P(("dp", "row"), "col"),
    )
    out_specs = P("row", "dp", "col")
    return jax.shard_map(
        on_device, mesh=mesh, in_specs=in_specs, out_specs=out_specs, check_vma=False
    )
```

profile of v0, /device:TPU:1, one launch (start us, length us, event | category | flops | bytes accessed | tf_op | source)
XLA Modules:
  0.0 211.0 jit_solution(15205189420382269202)
XLA Ops:
  6.5 0.0 all-gather.2.cloned.1.call-start
  6.5 0.7 all-gather.2.cloned.1.call-update
  7.3 0.0 reduce-scatter.4.cloned.1.call-start
  7.3 5.6 %fusion.6 = bf16[480,3584]{1,0:T(8,128)(2,1)S(1)} fusion(bf16[480,3584]{1,0:T(8,128)(2,1)} %param.6, bf16[480,3584]{1,0:T(8,128)(2,1)} %param.7, bf16[480,3584]{1,0:T(8,128)(2,1)} %param.5), kind=kLoop, calls=%fused_computation.9 | loop fusion | flops 22364160 | bytes 13762560 | tf_op jit(solution)/shard_map/convert_element_type | solution.py:35
  12.9 0.4 broadcast_in_dim.3
  13.3 11.5 %all_to_all.5 = bf16[2,480,3584]{2,1,0:T(8,128)(2,1)} all-to-all(bf16[2,480,3584]{2,1,0:T(8,128)(2,1)S(1)} %broadcast_in_dim.3), channel_id=1, replica_groups=mesh['dp'=16,'row'=2,'col'=4] {'row'}, dimensions={0} | all-to-all | bytes 13762560 | tf_op jit(solution)/shard_map/all_to_all | solution.py:9
  24.8 33.5 %all-gather.2.cloned.1.call-done = bf16[960,2048]{1,0:T(8,128)(2,1)} async-done(((bf16[240,2048]{1,0:T(8,128)(2,1)}), bf16[960,2048]{1,0:T(8,128)(2,1)}) %all-gather.2.cloned.1.call-update) | async-done | bytes 3932176 | tf_op jit(solution)/shard_map/all_gather | solution.py:30
  58.3 21.9 %fusion = bf16[2048,3584]{0,1:T(8,128)(2,1)} fusion(bf16[960,3584]{1,0:T(8,128)(2,1)} %bitcast.7, bf16[960,2048]{1,0:T(8,128)(2,1)} %all-gather.2.cloned.1.call-done), kind=kOutput, calls=%fused_computation.1 | convolution fusion | flops 14100201472 | bytes 25493504 | tf_op jit(solution)/shard_map/dot_general | solution.py:24
  80.2 18.6 %copy.7 = bf16[2048,3584]{1,0:T(8,128)(2,1)} copy(bf16[2048,3584]{0,1:T(8,128)(2,1)} %fusion) | data formatting | bytes 29360128
  98.8 0.0 reduce-scatter.4.cloned.1.call-update
  98.9 102.5 %reduce-scatter.4.cloned.1.call-done = bf16[128,3584]{1,0:T(8,128)(2,1)} async-done(((bf16[2048,3584]{1,0:T(8,128)(2,1)}), bf16[128,3584]{1,0:T(8,128)(2,1)}) %reduce-scatter.4.cloned.1.call-update) | async-done | bytes 917520
  201.4 1.5 copy.8
  202.9 1.3 copy.6
Async XLA Ops:
  6.5 51.8 %all-gather.2.cloned.1.call-start = ((), (), s32[]{:S(2)}) async-start(), calls=%async_computation.2 | async-start | bytes 4915200 | tf_op jit(solution)/shard_map/all_gather | solution.py:30
  7.3 194.1 %reduce-scatter.4.cloned.1.call-start = ((), (), s32[]{:S(2)}) async-start(), calls=%async_computation.3 | async-start | bytes 15597568
Sparse Core Ops, SparseCore 0:
  9.0 49.2 all-gather.1
  99.0 102.3 reduce-scatter.3
where the time goes:
time: 212 us; the launch traced here: 211 us
  waiting for transfers between devices  137 us (65%)
  local copies, waits for them, and re-layouts  21.9 us (10%)
  matrix products  21.9 us (10%)
  between operations  13.4 us (6%)
  blocking collectives  11.5 us (5%)
  other arithmetic  5.55 us (3%)
    unnamed x3, waiting for transfers between devices  103 us
    all_gather x1, waiting for transfers between devices, on_device(): tok_full = lax.all_gather(tokens, 'col', axis=0, tiled=True)  33.5 us
    dot_general x1, matrix products, contract_rows(): lax.dot_general(left, right, (((0,), (0,)), ((), ())), preferred_element_...  21.9 us
    unnamed x2, local copies, waits for them, and re-layouts  20.2 us
    all_to_all x1, blocking collectives, copy_for_each(): return lax.all_to_all(copies, axis, split_axis=0, concat_axis=0, tiled=True)  11.5 us
    convert_element_type x1, other arithmetic, on_device(): (cot_val * up_val * sigma * (1.0 + gate_val * (1.0 - sigma))).astype(jnp....  5.55 us
  transfers between devices with their start and end apart: 2, of which 2 were waited for; matrix products, arithmetic and copies ran while one was open for 3% of the time, Pallas kernels for 0%

commit v1 on v0

--- a/solution.py
+++ b/solution.py
@@ -27,7 +27,8 @@
 
 
 def on_device(tokens, hidden_cot, gate_pre, up_pre):
-    tok_full = lax.all_gather(tokens, "col", axis=0, tiled=True)
+    a_now = jnp.concatenate([tokens for _ in range(lax.axis_size("col"))], axis=0)
+    tok_full = lax.all_to_all(a_now, "col", 0, 0, tiled=True)
     gate_val = gate_pre.astype(jnp.float32)
     up_val = up_pre.astype(jnp.float32)
     cot_val = hidden_cot.astype(jnp.float32)

time: 212 us -> 211 us (level)
  blocking collectives: 11.5 us -> 50.3 us
  waiting for transfers between devices: 137 us -> 107 us
  local copies, waits for them, and re-layouts: 21.9 us -> 3.26 us
  starting transfers between devices: 0.04 us -> 7.95 us
  other arithmetic: 5.55 us -> 7.77 us
    unnamed x3 -> x1, waiting for transfers between devices: 103 us -> 0.02 us
    reduce_scatter x0 -> x1, waiting for transfers between devices: none -> 103 us  [on_device(): lax.psum_scatter(group_part.astype(jnp.bfloat16), 'dp', scatter_dimension...]
    all_to_all x1, blocking collectives: 11.5 us -> 50.3 us  [on_device(): tok_full = lax.all_to_all(a_now, 'col', 0, 0, tiled=True)]
    all_gather x1 -> x0, waiting for transfers between devices: 33.5 us -> none  [on_device(): tok_full = lax.all_gather(tokens, 'col', axis=0, tiled=True)]
    unnamed x2, local copies, waits for them, and re-layouts: 20.2 us -> 0.01 us
    all_to_all x0 -> x1, starting transfers between devices: none -> 7.95 us  [copy_for_each(): return lax.all_to_all(copies, axis, split_axis=0, concat_axis=0, tiled=True)]
    all_to_all x0 -> x1, waiting for transfers between devices: none -> 3.82 us  [copy_for_each(): return lax.all_to_all(copies, axis, split_axis=0, concat_axis=0, tiled=True)]
    broadcast_in_dim x1, local copies, waits for them, and re-layouts: 0.44 us -> 3.26 us  [copy_for_each(): copies = jnp.broadcast_to(x, (lax.axis_size(axis), *x.shape))]
  transfers between devices with their start and end apart: 2 -> 2, of which waited for: 2 -> 2; matrix products, arithmetic and copies ran while one was open for 3% -> 1% of each run, Pallas kernels for 0% -> 0%
where the time goes in v1:
time: 211 us
  waiting for transfers between devices  107 us (51%)
  blocking collectives  50.3 us (24%)
  matrix products  20.9 us (10%)
  between operations  13.4 us (6%)
  starting transfers between devices  7.95 us (4%)
  other arithmetic  7.77 us (4%)
  local copies, waits for them, and re-layouts  3.26 us (2%)
    reduce_scatter x1, waiting for transfers between devices, on_device(): lax.psum_scatter(group_part.astype(jnp.bfloat16), 'dp', scatter_dimension...  103 us
    all_to_all x1, blocking collectives, on_device(): tok_full = lax.all_to_all(a_now, 'col', 0, 0, tiled=True)  50.3 us
    dot_general x1, matrix products, contract_rows(): lax.dot_general(left, right, (((0,), (0,)), ((), ())), preferred_element_...  20.9 us
    all_to_all x1, starting transfers between devices, copy_for_each(): return lax.all_to_all(copies, axis, split_axis=0, concat_axis=0, tiled=True)  7.95 us
    convert_element_type x1, other arithmetic, on_device(): (cot_val * up_val * sigma * (1.0 + gate_val * (1.0 - sigma))).astype(jnp....  5.55 us
  transfers between devices with their start and end apart: 2, of which 2 were waited for; matrix products, arithmetic and copies ran while one was open for 1% of the time, Pallas kernels for 0%

profile of v1, /device:TPU:1, one launch (start us, length us, event | category | flops | bytes accessed | tf_op | source)
XLA Modules:
  0.0 210.5 jit_solution(18097276510412270551)
XLA Ops:
  6.5 5.5 %fusion.5 = bf16[480,3584]{1,0:T(8,128)(2,1)S(1)} fusion(bf16[480,3584]{1,0:T(8,128)(2,1)} %param.6, bf16[480,3584]{1,0:T(8,128)(2,1)} %param.7, bf16[480,3584]{1,0:T(8,128)(2,1)} %param.5), kind=kLoop, calls=%fused_computation.8 | loop fusion | flops 22364160 | bytes 13762560 | tf_op jit(solution)/shard_map/convert_element_type | solution.py:36
  12.1 3.3 %broadcast_in_dim.3 = bf16[2,480,3584]{2,1,0:T(8,128)(2,1)} broadcast(bf16[480,3584]{1,0:T(8,128)(2,1)S(1)} %fusion.5), dimensions={1,2} | broadcast | bytes 10321920 | tf_op jit(solution)/shard_map/broadcast_in_dim | solution.py:8
  15.3 0.0 copy-start
  15.4 8.0 %all-to-all-start.1 = ((bf16[2,480,3584]{2,1,0:T(8,128)(2,1)}), bf16[2,480,3584]{2,1,0:T(8,128)(2,1)}, u32[]{:S(2)}, u32[]{:S(2)}) async-start(bf16[2,480,3584]{2,1,0:T(8,128)(2,1)} %broadcast_in_dim.3), calls=%async_computation.1 | async-start | bytes 13762560 | tf_op jit(solution)/shard_map/all_to_all | solution.py:9
  23.3 0.0 reduce-scatter.2.cloned.1.call-start
  23.3 0.0 copy-done
  23.3 2.2 %pad_maximum_fusion = bf16[960,2048]{1,0:T(8,128)(2,1)} fusion(bf16[240,2048]{1,0:T(8,128)(2,1)S(1)} %copy-done), kind=kLoop, calls=%fused_computation.9 | loop fusion | flops 15728640 | bytes 4915200 | tf_op jit(solution)/shard_map/concatenate | solution.py:30
  25.5 3.8 %all-to-all-done.1 = bf16[2,480,3584]{2,1,0:T(8,128)(2,1)} async-done(((bf16[2,480,3584]{2,1,0:T(8,128)(2,1)}), bf16[2,480,3584]{2,1,0:T(8,128)(2,1)}, u32[]{:S(2)}, u32[]{:S(2)}) %all-to-all-start.1) | async-done | bytes 6881312 | tf_op jit(solution)/shard_map/all_to_all | solution.py:9
  29.4 50.3 %all_to_all.17 = bf16[4,240,2048]{2,1,0:T(8,128)(2,1)S(1)} all-to-all(bf16[4,240,2048]{2,1,0:T(8,128)(2,1)} %bitcast.6), channel_id=1, replica_groups=mesh['dp'=16,'row'=2,'col'=4] {'col'}, dimensions={0} | all-to-all | bytes 7864320 | tf_op jit(solution)/shard_map/all_to_all | solution.py:31
  79.6 20.9 %convolution_convert_fusion = bf16[2048,3584]{1,0:T(8,128)(2,1)} fusion(bf16[960,2048]{1,0:T(8,128)(2,1)S(1)} %bitcast.7, bf16[960,3584]{1,0:T(8,128)(2,1)} %bitcast.2), kind=kOutput, calls=%fused_computation | convolution fusion | flops 14100201472 | bytes 25493504 | tf_op jit(solution)/shard_map/dot_general | solution.py:24
  100.6 0.0 reduce-scatter.2.cloned.1.call-update
  100.6 103.1 %reduce-scatter.2.cloned.1.call-done = bf16[128,3584]{1,0:T(8,128)(2,1)} async-done(((bf16[2048,3584]{1,0:T(8,128)(2,1)}), bf16[128,3584]{1,0:T(8,128)(2,1)}) %reduce-scatter.2.cloned.1.call-update) | async-done | bytes 917520 | tf_op jit(solution)/shard_map/reduce_scatter | solution.py:38
Async XLA Ops:
  15.3 8.0 %copy-start = (bf16[240,2048]{1,0:T(8,128)(2,1)S(1)}, bf16[240,2048]{1,0:T(8,128)(2,1)}, u32[]{:S(2)}) copy-start(bf16[240,2048]{1,0:T(8,128)(2,1)} %param.4) | copy-start | bytes 2949124
  15.4 14.0 %all-to-all-start.1 = ((bf16[2,480,3584]{2,1,0:T(8,128)(2,1)}), bf16[2,480,3584]{2,1,0:T(8,128)(2,1)}, u32[]{:S(2)}, u32[]{:S(2)}) async-start(bf16[2,480,3584]{2,1,0:T(8,128)(2,1)} %broadcast_in_dim.3), calls=%async_computation.1 | async-start | bytes 13762560 | tf_op jit(solution)/shard_map/all_to_all | solution.py:9
  23.3 180.4 %reduce-scatter.2.cloned.1.call-start = ((), (), s32[]{:S(2)}) async-start(), calls=%async_computation.3 | async-start | bytes 15597568 | tf_op jit(solution)/shard_map/reduce_scatter | solution.py:38
Sparse Core Ops, SparseCore 0:
  100.7 102.9 reduce-scatter.1
